TPU v7x, 32 devices: a whole 2x2x4 slice. The times are simulated.
32 devices in a mesh: band: 4 (over y, x), ga: 8 (over z, core).
Axes of the slice: x: 2, y: 2, z: 4, core: 2. Of those that a mesh axis runs over, the one named last changes fastest.
Arguments:
- psi: float32 [4096, 4096], P('band', 'ga'), may hold values from -6 to 6
- lower: float32 [4096, 4096], P('band', 'ga'), as said below
Outputs:
- orthonormal: float32 [4096, 4096], P('band', 'ga')
- block_intersection: float32 [4096, 1024], P('band')
Inputs may be any that keep to these rules, and one draw needn't show every extreme that they name: lower is lower triangular with its diagonal between 1 and 2.
All inputs are finite; a program needn't handle non-finite values.
Results may differ from a plain program's by a relative error of at most 0.00022.
Values sent between devices are 32-bit elements; how exact they have to be, the bound alone decides.
A program may use at most 64 MiB of HBM per device.

v0:
```python
import functools

import jax
import jax.numpy as jnp
from jax import lax
from jax.experimental import pallas as pl
from jax.experimental.pallas import tpu as pltpu
from jax.sharding import PartitionSpec as P

MESH = pl.DeviceIdType.MESH
BASE = 128
PIECES = 4
CHUNKS = 8
ROWS = 4
F32 = jnp.float32
PAIRS = [(i, j) for i in range(ROWS) for j in range(i + 1)]
SHARE = len(PAIRS) // 2


def split(x):
    high = x.astype(jnp.bfloat16)
    return high, (x - high.astype(F32)).astype(jnp.bfloat16)


def dot(a, b, dims=((1,), (0,)), precision=None):
    return lax.dot_general(a, b, (dims, ((), ())), precision=precision, preferred_element_type=F32)


def mm3(a, b, dims=((1,), (0,))):
    return dot(a[0], b[0], dims) + (dot(a[0], b[1], dims) + dot(a[1], b[0], dims))


def exact(a, b):
    return dot(a, b, precision=lax.Precision.HIGHEST)


def kernel(
    bands, line, psi_ref, low_ref, y_ref, g_ref,
    lbuf, acc, other, own, own_hi, own_lo, part_hi, part_lo, minv, inv_hi, inv_lo, work,
    gpart, gsib, gin, gcross, gout,
    l_recv, l_right, l_left, l_twin, y_recv, y_send, y_out, psi_sem, own_sem,
    twin_sem, gin_recv, cross_recv, in_send, gout_recv, out_send, twin_send,
):
    nrows, width = psi_ref.shape
    lw = low_ref.shape[1]
    rc, w, rb = nrows // CHUNKS, width // PIECES, nrows // ROWS
    b, ga = lax.axis_index("band"), lax.axis_index("ga")
    z, c = ga // 2, ga % 2
    last = bands - 1
    twin = z * 2 + 1 - c

    def remote(src, dst, send, recv, device):
        return pltpu.make_async_remote_copy(
            src_ref=src, dst_ref=dst, send_sem=send, recv_sem=recv,
            device_id=device, device_id_type=MESH,
        )

    def chunk(s, h, i):
        return lbuf.at[s, h, pl.ds(pl.multiple_of(i * rc, rc), rc)]

    def tile_copy(s, i, send, device, h=None):
        h = c if h is None else h
        return remote(chunk(s, h, i), chunk(s, h, i), send.at[s, i], l_recv.at[s, h, i], (b, device))

    def to_right(s, i):
        return tile_copy(s, i, l_right, jnp.minimum(ga + 2, 2 * line - 1))

    def to_left(s, i):
        return tile_copy(s, i, l_left, jnp.maximum(ga - 2, 0))

    def to_twin(s, i):
        return tile_copy(s, i, l_twin, twin)

    def needed(s, h, i):
        return jnp.logical_or(s != b, (i + 1) * rc > h * lw)

    load_own = pltpu.make_async_copy(low_ref, lbuf.at[z, c], own_sem.at[0])
    load_psi = [
        pltpu.make_async_copy(psi_ref.at[:, pl.ds(j * w, w)], acc.at[j], psi_sem.at[j])
        for j in range(PIECES)
    ]

    @pl.when(z <= b)
    def _():
        load_own.start()

    for copy in load_psi:
        copy.start()

    barrier = pltpu.get_barrier_semaphore()
    for device in (lax.rem(ga + 2, 2 * line), lax.rem(ga + 2 * line - 2, 2 * line), twin):
        pl.semaphore_signal(barrier, inc=1, device_id=(b, device), device_id_type=MESH)
    for d in range(1, bands):
        pl.semaphore_signal(barrier, inc=1, device_id=(lax.rem(b + d, bands), ga), device_id_type=MESH)
    pl.semaphore_wait(barrier, 2 + bands)

    @pl.when(z <= b)
    def _():
        load_own.wait()

        @pl.loop(0, CHUNKS)
        def _(i):
            @pl.when(needed(z, c, i))
            def _():
                to_twin(z, i).start()

    def right_tile(turn):
        s = jnp.where(b == last, turn, b if turn == 0 else turn - 1)
        live = jnp.where(b == last, turn < b, turn <= b)
        return s, jnp.logical_and(live, s <= z)

    def left_tile(turn):
        s = b - turn
        return s, s >= z

    def relay(turn, i):
        s, live = right_tile(turn)
        live = jnp.logical_and(live, needed(s, c, i))

        @pl.when(jnp.logical_and(live, s < z))
        def _():
            to_right(s, i).wait_recv()
            to_twin(s, i).start()

        @pl.when(jnp.logical_and(live, z < line - 1))
        def _():
            to_right(s, i).start()

        t, live = left_tile(turn)
        live = jnp.logical_and(live, needed(t, c, i))

        @pl.when(jnp.logical_and(live, t > z))
        def _():
            to_left(t, i).wait_recv()
            to_twin(t, i).start()

        @pl.when(jnp.logical_and(live, z > 0))
        def _():
            to_left(t, i).start()

    def relays(turn, first, count):
        @pl.loop(first, first + count)
        def _(i):
            relay(turn, i)

    def wait_twin(s):
        @pl.loop(0, CHUNKS)
        def _(i):
            @pl.when(needed(s, 1 - c, i))
            def _():
                tile_copy(s, i, l_twin, twin, 1 - c).wait_recv()

    blocks = nrows // BASE
    group = min(4, blocks)

    def invert_blocks(g):
        row = lax.broadcasted_iota(jnp.int32, (BASE, BASE), 0)
        col = lax.broadcasted_iota(jnp.int32, (BASE, BASE), 1)
        tiles, inverses = [], []
        for k in range(group):
            at = (g * group + k) * BASE
            tile = lbuf[b, at // lw, at : at + BASE, at % lw : at % lw + BASE]
            tiles.append(tile)
            inverses.append(jnp.where(row == col, 1.0 / jnp.where(row == col, tile, 1.0), 0.0))
        size = 1
        while size < BASE:
            off = (row // (2 * size) == col // (2 * size)) & (row // size > col // size)
            inner = [exact(jnp.where(off, t, 0.0), v) for t, v in zip(tiles, inverses)]
            inverses = [v - exact(v, u) for v, u in zip(inverses, inner)]
            size *= 2
        for k in range(group):
            at = (g * group + k) * BASE
            minv[at : at + BASE, at : at + BASE] = inverses[k]

    def merge_blocks():
        size = BASE
        while size < nrows:
            step = min(size, 256)
            for at in range(0, nrows, 2 * size):
                half, off = at // lw, at % lw
                first = split(minv[at : at + size, at : at + size])
                for r in range(0, size, step):
                    below = lbuf[b, half, at + size + r : at + size + r + step, off : off + size]
                    work[r : r + step, :size] = mm3(split(below), first)
                inner = split(work[:size, :size])
                for r in range(0, size, step):
                    rows = pl.ds(at + size + r, step)
                    second = minv[rows, at + size : at + 2 * size]
                    minv[rows, at : at + size] = -mm3(split(second), inner)
            size *= 2
        for r in range(ROWS):
            rows, depth = pl.ds(r * rb, rb), (r + 1) * rb
            value = minv[rows, :depth]
            at = lax.broadcasted_iota(jnp.int32, (rb, depth), 0) + r * rb
            value = jnp.where(at >= lax.broadcasted_iota(jnp.int32, (rb, depth), 1), value, 0.0)
            inv_hi[rows, :depth], inv_lo[rows, :depth] = split(value)

    def y_copy(s, j, d):
        return remote(
            own.at[j], other.at[s, j], y_send.at[d - 1, j], y_recv.at[s, j],
            (jnp.minimum(b + d, last), ga),
        )

    def update(s, pieces):
        for j in pieces:
            y_copy(s, j, 1).wait_recv()
            part_hi[j], part_lo[j] = split(other[s, j])

        @pl.loop(0, ROWS)
        def _(r):
            rows = pl.ds(pl.multiple_of(r * rb, rb), rb)
            for h in range(2):
                tile = split(lbuf[s, h, rows])
                for j in pieces:
                    cols = slice(h * lw, (h + 1) * lw)
                    acc[j, rows] -= mm3(tile, (part_hi[j, cols], part_lo[j, cols]))

    def apply_inverse(j):
        part_hi[j], part_lo[j] = split(acc[j])
        for r in range(ROWS):
            rows, depth = slice(r * rb, (r + 1) * rb), (r + 1) * rb
            value = mm3(
                (inv_hi[rows, :depth], inv_lo[rows, :depth]), (part_hi[j, :depth], part_lo[j, :depth])
            )
            own[j, rows] = value
            own_hi[j, rows], own_lo[j, rows] = split(value)

    def out_copy(j):
        return pltpu.make_async_copy(
            own.at[j], y_ref.at[:, pl.ds(pl.multiple_of(j * w, w), w)], y_out.at[j]
        )

    relays(0, 0, CHUNKS)
    wait_twin(b)
    groups = blocks // group
    for g in range(groups):
        relays(1, g * CHUNKS // groups, CHUNKS // groups)
        invert_blocks(g)
    merge_blocks()
    for copy in load_psi:
        copy.wait()
    for turn in range(2, bands - 1):
        if turn == 2:
            @pl.when(b >= 2)
            def _():
                wait_twin(0)
                update(0, range(PIECES))

        relays(turn, 0, CHUNKS)
    for s in range(1, bands - 2):
        @pl.when(b >= s + 2)
        def _():
            wait_twin(s)
            update(s, range(PIECES))

    @pl.when(b > 0)
    def _():
        wait_twin(b - 1)

    gpart[...] = jnp.zeros_like(gpart)

    @pl.loop(0, PIECES)
    def _(j):
        @pl.when(b > 0)
        def _():
            update(b - 1, [j])

        apply_inverse(j)
        for d in range(1, bands):
            @pl.when(b + d < bands)
            def _():
                y_copy(b, j, d).start()

        out_copy(j).start()
        for k, (p, q) in enumerate(PAIRS):
            up, left = slice(p * rb, (p + 1) * rb), slice(q * rb, (q + 1) * rb)
            gpart[k] += mm3(
                (own_hi[j, up], own_lo[j, up]), (own_hi[j, left], own_lo[j, left]), ((1,), (1,))
            )

    mine = c * SHARE
    to_sib = remote(
        gpart.at[pl.ds((1 - c) * SHARE, SHARE)], gsib, twin_sem.at[0], twin_sem.at[1], (b, twin)
    )
    to_sib.start()
    lower_half = z < line // 2
    inward = jnp.where(lower_half, ga + 2, ga - 2)
    has_out = jnp.where(lower_half, z > 0, z < line - 1)
    outward = jnp.where(has_out, jnp.where(lower_half, ga - 2, ga + 2), inward)
    middle = jnp.where(lower_half, z == line // 2 - 1, z == line // 2)

    def in_copy(k):
        return remote(gpart.at[mine + k], gin.at[k], in_send.at[k], gin_recv.at[k], (b, inward))

    def cross_copy(k):
        return remote(gpart.at[mine + k], gcross.at[k], in_send.at[k], cross_recv.at[k], (b, inward))

    def back_copy(k):
        return remote(
            gout.at[mine + k], gout.at[mine + k], out_send.at[k], gout_recv.at[mine + k], (b, outward)
        )

    def share_copy(k, base):
        return remote(
            gout.at[base + k], gout.at[base + k], twin_send.at[k], gout_recv.at[base + k], (b, twin)
        )

    to_sib.wait_recv()

    @pl.loop(0, SHARE)
    def _(k):
        gpart[mine + k] += gsib[k]

        @pl.when(has_out)
        def _():
            in_copy(k).wait_recv()
            gpart[mine + k] += gin[k]

        @pl.when(middle)
        def _():
            cross_copy(k).start()

        @pl.when(jnp.logical_not(middle))
        def _():
            in_copy(k).start()

    @pl.loop(0, SHARE)
    def _(k):
        @pl.when(middle)
        def _():
            cross_copy(k).wait_recv()
            gout[mine + k] = gpart[mine + k] + gcross[k]

        @pl.when(jnp.logical_not(middle))
        def _():
            back_copy(k).wait_recv()

        @pl.when(has_out)
        def _():
            back_copy(k).start()

        share_copy(k, mine).start()

    theirs = (1 - c) * SHARE

    @pl.loop(0, SHARE)
    def _(k):
        share_copy(k, theirs).wait_recv()

    scale = 1.0 / (width * 2 * line)
    for k, (p, q) in enumerate(PAIRS):
        value = gout[k] * scale
        g_ref[p * rb : (p + 1) * rb, q * rb : (q + 1) * rb] = value
        if p != q:
            g_ref[q * rb : (q + 1) * rb, p * rb : (p + 1) * rb] = value.T

    for turn in range(bands - 1):
        @pl.loop(0, CHUNKS)
        def _(i):
            s, live = right_tile(turn)
            live = jnp.logical_and(live, needed(s, c, i))

            @pl.when(jnp.logical_and(live, z < line - 1))
            def _():
                to_right(s, i).wait_send()

            @pl.when(jnp.logical_and(live, s < z))
            def _():
                to_twin(s, i).wait_send()

            t, live = left_tile(turn)
            live = jnp.logical_and(live, needed(t, c, i))

            @pl.when(jnp.logical_and(live, z > 0))
            def _():
                to_left(t, i).wait_send()

            @pl.when(jnp.logical_and(live, t > z))
            def _():
                to_twin(t, i).wait_send()

    @pl.when(z <= b)
    def _():
        @pl.loop(0, CHUNKS)
        def _(i):
            @pl.when(needed(z, c, i))
            def _():
                to_twin(z, i).wait_send()

    @pl.loop(0, PIECES)
    def _(j):
        for d in range(1, bands):
            @pl.when(b + d < bands)
            def _():
                y_copy(b, j, d).wait_send()

        out_copy(j).wait()

    to_sib.wait_send()

    @pl.loop(0, SHARE)
    def _(k):
        in_copy(k).wait_send()
        share_copy(k, mine).wait_send()

        @pl.when(has_out)
        def _():
            back_copy(k).wait_send()


def solution(mesh):
    bands, line = mesh.shape["band"], mesh.shape["ga"] // 2

    def local(psi, lower):
        nrows, width = psi.shape
        lw = lower.shape[1]
        w, rb = width // PIECES, nrows // ROWS
        vmem, dma = pltpu.VMEM, pltpu.SemaphoreType.DMA
        bf16 = jnp.bfloat16
        share = (SHARE, rb, rb)
        return pl.pallas_call(
            functools.partial(kernel, bands, line),
            out_shape=(
                jax.ShapeDtypeStruct((nrows, width), F32),
                jax.ShapeDtypeStruct((nrows, nrows), F32),
            ),
            in_specs=[pl.BlockSpec(memory_space=pl.ANY)] * 2,
            out_specs=(pl.BlockSpec(memory_space=pl.ANY), pl.BlockSpec(memory_space=pltpu.VMEM)),
            scratch_shapes=[
                vmem((bands, 2, nrows, lw), F32),
                vmem((PIECES, nrows, w), F32),
                vmem((bands - 1, PIECES, nrows, w), F32),
                vmem((PIECES, nrows, w), F32),
                vmem((PIECES, nrows, w), bf16),
                vmem((PIECES, nrows, w), bf16),
                vmem((PIECES, nrows, w), bf16),
                vmem((PIECES, nrows, w), bf16),
                vmem((nrows, nrows), F32),
                vmem((nrows, nrows), bf16),
                vmem((nrows, nrows), bf16),
                vmem((nrows // 2, nrows // 2), F32),
                vmem((2 * SHARE, rb, rb), F32),
                vmem(share, F32),
                vmem(share, F32),
                vmem(share, F32),
                vmem((2 * SHARE, rb, rb), F32),
                dma((bands, 2, CHUNKS)),
                dma((bands, CHUNKS)),
                dma((bands, CHUNKS)),
                dma((bands, CHUNKS)),
                dma((bands - 1, PIECES)),
                dma((bands - 1, PIECES)),
                dma((PIECES,)),
                dma((PIECES,)),
                dma((1,)),
                dma((2,)),
                dma((SHARE,)),
                dma((SHARE,)),
                dma((SHARE,)),
                dma((2 * SHARE,)),
                dma((SHARE,)),
                dma((SHARE,)),
            ],
            compiler_params=pltpu.CompilerParams(
                collective_id=0, has_side_effects=True, vmem_limit_bytes=63 * 1024 * 1024
            ),
        )(psi, lower)

    return jax.shard_map(
        local,
        mesh=mesh,
        in_specs=(P("band", "ga"), P("band", "ga")),
        out_specs=(P("band", "ga"), P("band", None)),
        check_vma=False,
    )
```

profile of v0, /device:TPU:7, one launch (start us, length us, event | category | flops | bytes accessed | tf_op | source)
XLA Modules:
  0.0 532.2 jit_solution(9059037610460985291)
XLA Ops:
  0.6 526.3 %shard_map.41 = (f32[1024,512]{1,0:T(8,128)}, f32[1024,1024]{1,0:T(8,128)}) custom-call(f32[1024,512]{1,0:T(8,128)} %psi_ref.1, f32[1024,512]{1,0:T(8,128)} %low_ref.1), custom_call_target="tpu_custom_call" | custom-call | tf_op jit(solution)/shard_map/pallas_call | solution.py:421
  526.9 0.0 copy-start
  526.9 3.2 copy.6
  530.2 0.0 copy-done
  530.2 2.0 copy.7
Async XLA Ops:
  526.9 3.2 copy-start
where the time goes:
time: 532 us
  Pallas kernels  526 us (99%)
    pallas_call x1, Pallas kernels, local(): pl.pallas_call(functools.partial(kernel, bands, line), out_shape=(jax.Sha...  526 us

commit v1 on v0

--- a/solution.py
+++ b/solution.py
@@ -11,10 +11,11 @@
 BASE = 128
 PIECES = 4
 CHUNKS = 8
+SKEW = 2
 ROWS = 4
 F32 = jnp.float32
 PAIRS = [(i, j) for i in range(ROWS) for j in range(i + 1)]
-SHARE = len(PAIRS) // 2
+SHARE = len(PAIRS)
 
 
 def split(x):
@@ -46,7 +47,8 @@
     rc, w, rb = nrows // CHUNKS, width // PIECES, nrows // ROWS
     b, ga = lax.axis_index("band"), lax.axis_index("ga")
     z, c = ga // 2, ga % 2
-    last = bands - 1
+    last, turns = bands - 1, bands - 1
+    drain = SKEW * (line - 1)
     twin = z * 2 + 1 - c
 
     def remote(src, dst, send, recv, device):
@@ -105,7 +107,7 @@
                 to_twin(z, i).start()
 
     def right_tile(turn):
-        s = jnp.where(b == last, turn, b if turn == 0 else turn - 1)
+        s = jnp.where(b == last, turn, jnp.where(turn == 0, b, turn - 1))
         live = jnp.where(b == last, turn < b, turn <= b)
         return s, jnp.logical_and(live, s <= z)
 
@@ -113,35 +115,37 @@
         s = b - turn
         return s, s >= z
 
-    def relay(turn, i):
-        s, live = right_tile(turn)
-        live = jnp.logical_and(live, needed(s, c, i))
-
-        @pl.when(jnp.logical_and(live, s < z))
-        def _():
-            to_right(s, i).wait_recv()
-            to_twin(s, i).start()
-
-        @pl.when(jnp.logical_and(live, z < line - 1))
-        def _():
-            to_right(s, i).start()
-
-        t, live = left_tile(turn)
-        live = jnp.logical_and(live, needed(t, c, i))
-
-        @pl.when(jnp.logical_and(live, t > z))
-        def _():
-            to_left(t, i).wait_recv()
-            to_twin(t, i).start()
-
-        @pl.when(jnp.logical_and(live, z > 0))
-        def _():
-            to_left(t, i).start()
-
-    def relays(turn, first, count):
+    def stream(tick, hops, tile, moves, send):
+        @pl.when(jnp.logical_and(tick >= hops * SKEW, tick < hops * SKEW + turns * CHUNKS))
+        def _():
+            step = tick - hops * SKEW
+            turn, i = step // CHUNKS, step % CHUNKS
+            s, live = tile(turn)
+            s = jnp.clip(s, 0, last)
+
+            @pl.when(jnp.logical_and(jnp.logical_and(live, s == z), jnp.logical_and(moves, i == 0)))
+            def _():
+                @pl.loop(0, CHUNKS)
+                def _(k):
+                    @pl.when(needed(z, c, k))
+                    def _():
+                        send(z, k).start()
+
+            @pl.when(jnp.logical_and(jnp.logical_and(live, s != z), needed(s, c, i)))
+            def _():
+                send(s, i).wait_recv()
+
+                @pl.when(moves)
+                def _():
+                    send(s, i).start()
+
+                to_twin(s, i).start()
+
+    def ticks(first, count):
         @pl.loop(first, first + count)
-        def _(i):
-            relay(turn, i)
+        def _(tick):
+            stream(tick, z, right_tile, z < line - 1, to_right)
+            stream(tick, line - 1 - z, left_tile, z > 0, to_left)
 
     def wait_twin(s):
         @pl.loop(0, CHUNKS)
@@ -201,9 +205,23 @@
             (jnp.minimum(b + d, last), ga),
         )
 
+    def direct(d):
+        reaches = b + d < bands
+        return jnp.logical_and(reaches, b > 0) if d == last else reaches
+
+    def pass_on(j):
+        return remote(
+            other.at[0, j], other.at[0, j], y_send.at[1, j], y_recv.at[0, j], (b * 0 + last, ga)
+        )
+
     def update(s, pieces):
         for j in pieces:
             y_copy(s, j, 1).wait_recv()
+            if isinstance(s, int) and s == 0:
+                @pl.when(b == last - 1)
+                def _():
+                    pass_on(j).start()
+
             part_hi[j], part_lo[j] = split(other[s, j])
 
         @pl.loop(0, ROWS)
@@ -230,11 +248,11 @@
             own.at[j], y_ref.at[:, pl.ds(pl.multiple_of(j * w, w), w)], y_out.at[j]
         )
 
-    relays(0, 0, CHUNKS)
+    ticks(0, CHUNKS + drain)
     wait_twin(b)
     groups = blocks // group
     for g in range(groups):
-        relays(1, g * CHUNKS // groups, CHUNKS // groups)
+        ticks(CHUNKS + drain + g * CHUNKS // groups, CHUNKS // groups)
         invert_blocks(g)
     merge_blocks()
     for copy in load_psi:
@@ -246,7 +264,7 @@
                 wait_twin(0)
                 update(0, range(PIECES))
 
-        relays(turn, 0, CHUNKS)
+        ticks(turn * CHUNKS + drain, CHUNKS)
     for s in range(1, bands - 2):
         @pl.when(b >= s + 2)
         def _():
@@ -267,16 +285,18 @@
 
         apply_inverse(j)
         for d in range(1, bands):
-            @pl.when(b + d < bands)
+            @pl.when(direct(d))
             def _():
                 y_copy(b, j, d).start()
 
         out_copy(j).start()
         for k, (p, q) in enumerate(PAIRS):
             up, left = slice(p * rb, (p + 1) * rb), slice(q * rb, (q + 1) * rb)
-            gpart[k] += mm3(
+            value = mm3(
                 (own_hi[j, up], own_lo[j, up]), (own_hi[j, left], own_lo[j, left]), ((1,), (1,))
             )
+            gpart[2 * k] += value[: rb // 2]
+            gpart[2 * k + 1] += value[rb // 2 :]
 
     mine = c * SHARE
     to_sib = remote(
@@ -307,8 +327,7 @@
 
     to_sib.wait_recv()
 
-    @pl.loop(0, SHARE)
-    def _(k):
+    def inward_leg(k):
         gpart[mine + k] += gsib[k]
 
         @pl.when(has_out)
@@ -324,8 +343,7 @@
         def _():
             in_copy(k).start()
 
-    @pl.loop(0, SHARE)
-    def _(k):
+    def outward_leg(k):
         @pl.when(middle)
         def _():
             cross_copy(k).wait_recv()
@@ -340,6 +358,18 @@
             back_copy(k).start()
 
         share_copy(k, mine).start()
+
+    lag = jnp.where(middle, 2, SHARE)
+
+    @pl.loop(0, 2 * SHARE)
+    def _(k):
+        @pl.when(k < SHARE)
+        def _():
+            inward_leg(k)
+
+        @pl.when(jnp.logical_and(k >= lag, k < SHARE + lag))
+        def _():
+            outward_leg(k - lag)
 
     theirs = (1 - c) * SHARE
 
@@ -349,7 +379,7 @@
 
     scale = 1.0 / (width * 2 * line)
     for k, (p, q) in enumerate(PAIRS):
-        value = gout[k] * scale
+        value = jnp.concatenate([gout[2 * k], gout[2 * k + 1]], axis=0) * scale
         g_ref[p * rb : (p + 1) * rb, q * rb : (q + 1) * rb] = value
         if p != q:
             g_ref[q * rb : (q + 1) * rb, p * rb : (p + 1) * rb] = value.T
@@ -358,6 +388,7 @@
         @pl.loop(0, CHUNKS)
         def _(i):
             s, live = right_tile(turn)
+            s = jnp.clip(s, 0, last)
             live = jnp.logical_and(live, needed(s, c, i))
 
             @pl.when(jnp.logical_and(live, z < line - 1))
@@ -369,6 +400,7 @@
                 to_twin(s, i).wait_send()
 
             t, live = left_tile(turn)
+            t = jnp.clip(t, 0, last)
             live = jnp.logical_and(live, needed(t, c, i))
 
             @pl.when(jnp.logical_and(live, z > 0))
@@ -390,9 +422,13 @@
     @pl.loop(0, PIECES)
     def _(j):
         for d in range(1, bands):
-            @pl.when(b + d < bands)
+            @pl.when(direct(d))
             def _():
                 y_copy(b, j, d).wait_send()
+
+        @pl.when(b == last - 1)
+        def _():
+            pass_on(j).wait_send()
 
         out_copy(j).wait()
 
@@ -417,7 +453,7 @@
         w, rb = width // PIECES, nrows // ROWS
         vmem, dma = pltpu.VMEM, pltpu.SemaphoreType.DMA
         bf16 = jnp.bfloat16
-        share = (SHARE, rb, rb)
+        share = (SHARE, rb // 2, rb)
         return pl.pallas_call(
             functools.partial(kernel, bands, line),
             out_shape=(
@@ -439,11 +475,11 @@
                 vmem((nrows, nrows), bf16),
                 vmem((nrows, nrows), bf16),
                 vmem((nrows // 2, nrows // 2), F32),
-                vmem((2 * SHARE, rb, rb), F32),
+                vmem((2 * SHARE, rb // 2, rb), F32),
                 vmem(share, F32),
                 vmem(share, F32),
                 vmem(share, F32),
-                vmem((2 * SHARE, rb, rb), F32),
+                vmem((2 * SHARE, rb // 2, rb), F32),
                 dma((bands, 2, CHUNKS)),
                 dma((bands, CHUNKS)),
                 dma((bands, CHUNKS)),

time: 532 us -> 310 us (0.58)
  Pallas kernels: 526 us -> 304 us
    pallas_call x1, Pallas kernels: 526 us -> 304 us  [local(): pl.pallas_call(functools.partial(kernel, bands, line), out_shape=(jax.Sha...]
where the time goes in v1:
time: 310 us
  Pallas kernels  304 us (98%)
  local copies, waits for them, and re-layouts  5.25 us (2%)
    pallas_call x1, Pallas kernels, local(): pl.pallas_call(functools.partial(kernel, bands, line), out_shape=(jax.Sha...  304 us

profile of v1, /device:TPU:7, one launch (start us, length us, event | category | flops | bytes accessed | tf_op | source)
XLA Modules:
  0.0 310.2 jit_solution(15213563079926333081)
XLA Ops:
  0.6 304.3 %shard_map.41 = (f32[1024,512]{1,0:T(8,128)}, f32[1024,1024]{1,0:T(8,128)}) custom-call(f32[1024,512]{1,0:T(8,128)} %psi_ref.1, f32[1024,512]{1,0:T(8,128)} %low_ref.1), custom_call_target="tpu_custom_call" | custom-call | tf_op jit(solution)/shard_map/pallas_call | solution.py:457
  304.9 0.0 copy-start
  304.9 3.2 %copy.6 = f32[1024,512]{1,0:T(8,128)} copy(f32[1024,512]{1,0:T(8,128)} %get-tuple-element.4) | data formatting | bytes 4194304
  308.2 0.0 copy-done
  308.2 2.0 copy.7
Async XLA Ops:
  304.9 3.2 %copy-start = (f32[1024,1024]{1,0:T(8,128)S(1)}, f32[1024,1024]{1,0:T(8,128)}, u32[]{:S(2)}) copy-start(f32[1024,1024]{1,0:T(8,128)} %get-tuple-element.5) | copy-start | bytes 12582916

commit v2 on v1

--- a/solution.py
+++ b/solution.py
@@ -23,16 +23,12 @@
     return high, (x - high.astype(F32)).astype(jnp.bfloat16)
 
 
-def dot(a, b, dims=((1,), (0,)), precision=None):
-    return lax.dot_general(a, b, (dims, ((), ())), precision=precision, preferred_element_type=F32)
+def dot(a, b, dims=((1,), (0,))):
+    return lax.dot_general(a, b, (dims, ((), ())), preferred_element_type=F32)
 
 
 def mm3(a, b, dims=((1,), (0,))):
     return dot(a[0], b[0], dims) + (dot(a[0], b[1], dims) + dot(a[1], b[0], dims))
-
-
-def exact(a, b):
-    return dot(a, b, precision=lax.Precision.HIGHEST)
 
 
 def kernel(
@@ -169,8 +165,9 @@
         size = 1
         while size < BASE:
             off = (row // (2 * size) == col // (2 * size)) & (row // size > col // size)
-            inner = [exact(jnp.where(off, t, 0.0), v) for t, v in zip(tiles, inverses)]
-            inverses = [v - exact(v, u) for v, u in zip(inverses, inner)]
+            parts = [split(v) for v in inverses]
+            inner = [mm3(split(jnp.where(off, t, 0.0)), v) for t, v in zip(tiles, parts)]
+            inverses = [v - mm3(p, split(u)) for v, p, u in zip(inverses, parts, inner)]
             size *= 2
         for k in range(group):
             at = (g * group + k) * BASE
@@ -209,18 +206,9 @@
         reaches = b + d < bands
         return jnp.logical_and(reaches, b > 0) if d == last else reaches
 
-    def pass_on(j):
-        return remote(
-            other.at[0, j], other.at[0, j], y_send.at[1, j], y_recv.at[0, j], (b * 0 + last, ga)
-        )
-
     def update(s, pieces):
         for j in pieces:
             y_copy(s, j, 1).wait_recv()
-            if isinstance(s, int) and s == 0:
-                @pl.when(b == last - 1)
-                def _():
-                    pass_on(j).start()
 
             part_hi[j], part_lo[j] = split(other[s, j])
 
@@ -258,18 +246,11 @@
     for copy in load_psi:
         copy.wait()
     for turn in range(2, bands - 1):
-        if turn == 2:
-            @pl.when(b >= 2)
-            def _():
-                wait_twin(0)
-                update(0, range(PIECES))
-
         ticks(turn * CHUNKS + drain, CHUNKS)
-    for s in range(1, bands - 2):
-        @pl.when(b >= s + 2)
-        def _():
-            wait_twin(s)
-            update(s, range(PIECES))
+    @pl.loop(0, b - 1)
+    def _(s):
+        wait_twin(s)
+        update(s, range(PIECES))
 
     @pl.when(b > 0)
     def _():
@@ -297,6 +278,11 @@
             )
             gpart[2 * k] += value[: rb // 2]
             gpart[2 * k + 1] += value[rb // 2 :]
+
+    @pl.when(b == 0)
+    def _():
+        for j in range(PIECES):
+            y_copy(b, j, last).start()
 
     mine = c * SHARE
     to_sib = remote(
@@ -426,9 +412,9 @@
             def _():
                 y_copy(b, j, d).wait_send()
 
-        @pl.when(b == last - 1)
-        def _():
-            pass_on(j).wait_send()
+        @pl.when(b == 0)
+        def _():
+            y_copy(b, j, last).wait_send()
 
         out_copy(j).wait()
 

time: 310 us -> 278 us (0.90)
  Pallas kernels: 304 us -> 272 us
    pallas_call x1, Pallas kernels: 304 us -> 272 us  [local(): pl.pallas_call(functools.partial(kernel, bands, line), out_shape=(jax.Sha...]
where the time goes in v2:
time: 278 us
  Pallas kernels  272 us (98%)
  local copies, waits for them, and re-layouts  5.25 us (2%)
    pallas_call x1, Pallas kernels, local(): pl.pallas_call(functools.partial(kernel, bands, line), out_shape=(jax.Sha...  272 us

profile of v2, /device:TPU:7, one launch (start us, length us, event | category | flops | bytes accessed | tf_op | source)
XLA Modules:
  0.0 278.2 jit_solution(3485512092630031225)
XLA Ops:
  0.6 272.3 %shard_map.41 = (f32[1024,512]{1,0:T(8,128)}, f32[1024,1024]{1,0:T(8,128)}) custom-call(f32[1024,512]{1,0:T(8,128)} %psi_ref.1, f32[1024,512]{1,0:T(8,128)} %low_ref.1), custom_call_target="tpu_custom_call" | custom-call | tf_op jit(solution)/shard_map/pallas_call | solution.py:443
  273.0 0.0 copy-start
  273.0 3.2 %copy.6 = f32[1024,512]{1,0:T(8,128)} copy(f32[1024,512]{1,0:T(8,128)} %get-tuple-element.4) | data formatting | bytes 4194304
  276.2 0.0 copy-done
  276.2 2.0 copy.7
Async XLA Ops:
  273.0 3.2 %copy-start = (f32[1024,1024]{1,0:T(8,128)S(1)}, f32[1024,1024]{1,0:T(8,128)}, u32[]{:S(2)}) copy-start(f32[1024,1024]{1,0:T(8,128)} %get-tuple-element.5) | copy-start | bytes 12582916

commit v3 on v2

--- a/solution.py
+++ b/solution.py
@@ -53,24 +53,29 @@
             device_id=device, device_id_type=MESH,
         )
 
-    def chunk(s, h, i):
-        return lbuf.at[s, h, pl.ds(pl.multiple_of(i * rc, rc), rc)]
-
-    def tile_copy(s, i, send, device, h=None):
+    def chunk(s, h, i, wide):
+        rows = pl.ds(pl.multiple_of(i * rc, rc), rc)
+        return lbuf.at[s, h, rows, pl.ds(0, wide)]
+
+    def tile_copy(s, i, send, device, wide, h=None):
         h = c if h is None else h
-        return remote(chunk(s, h, i), chunk(s, h, i), send.at[s, i], l_recv.at[s, h, i], (b, device))
-
-    def to_right(s, i):
-        return tile_copy(s, i, l_right, jnp.minimum(ga + 2, 2 * line - 1))
-
-    def to_left(s, i):
-        return tile_copy(s, i, l_left, jnp.maximum(ga - 2, 0))
-
-    def to_twin(s, i):
-        return tile_copy(s, i, l_twin, twin)
-
-    def needed(s, h, i):
-        return jnp.logical_or(s != b, (i + 1) * rc > h * lw)
+        part = chunk(s, h, i, wide)
+        return remote(part, part, send.at[s, i], l_recv.at[s, h, i], (b, device))
+
+    def to_right(s, i, wide):
+        return tile_copy(s, i, l_right, jnp.minimum(ga + 2, 2 * line - 1), wide)
+
+    def to_left(s, i, wide):
+        return tile_copy(s, i, l_left, jnp.maximum(ga - 2, 0), wide)
+
+    def to_twin(s, i, wide):
+        return tile_copy(s, i, l_twin, twin, wide)
+
+    def sizes(s, h, i, on=True):
+        lanes = 128
+        reach = jnp.minimum(((i + 1) * rc - h * lw + lanes - 1) // lanes, lw // lanes)
+        count = jnp.where(s == b, reach, lw // lanes)
+        return [(m * lanes, jnp.logical_and(on, count == m)) for m in range(1, lw // lanes + 1)]
 
     load_own = pltpu.make_async_copy(low_ref, lbuf.at[z, c], own_sem.at[0])
     load_psi = [
@@ -98,9 +103,10 @@
 
         @pl.loop(0, CHUNKS)
         def _(i):
-            @pl.when(needed(z, c, i))
-            def _():
-                to_twin(z, i).start()
+            for wide, on in sizes(z, c, i):
+                @pl.when(on)
+                def _():
+                    to_twin(z, i, wide).start()
 
     def right_tile(turn):
         s = jnp.where(b == last, turn, jnp.where(turn == 0, b, turn - 1))
@@ -123,19 +129,21 @@
             def _():
                 @pl.loop(0, CHUNKS)
                 def _(k):
-                    @pl.when(needed(z, c, k))
+                    for wide, on in sizes(z, c, k):
+                        @pl.when(on)
+                        def _():
+                            send(z, k, wide).start()
+
+            for wide, on in sizes(s, c, i, jnp.logical_and(live, s != z)):
+                @pl.when(on)
+                def _():
+                    send(s, i, wide).wait_recv()
+
+                    @pl.when(moves)
                     def _():
-                        send(z, k).start()
-
-            @pl.when(jnp.logical_and(jnp.logical_and(live, s != z), needed(s, c, i)))
-            def _():
-                send(s, i).wait_recv()
-
-                @pl.when(moves)
-                def _():
-                    send(s, i).start()
-
-                to_twin(s, i).start()
+                        send(s, i, wide).start()
+
+                    to_twin(s, i, wide).start()
 
     def ticks(first, count):
         @pl.loop(first, first + count)
@@ -146,9 +154,10 @@
     def wait_twin(s):
         @pl.loop(0, CHUNKS)
         def _(i):
-            @pl.when(needed(s, 1 - c, i))
-            def _():
-                tile_copy(s, i, l_twin, twin, 1 - c).wait_recv()
+            for wide, on in sizes(s, 1 - c, i):
+                @pl.when(on)
+                def _():
+                    tile_copy(s, i, l_twin, twin, wide, 1 - c).wait_recv()
 
     blocks = nrows // BASE
     group = min(4, blocks)
@@ -247,22 +256,24 @@
         copy.wait()
     for turn in range(2, bands - 1):
         ticks(turn * CHUNKS + drain, CHUNKS)
-    @pl.loop(0, b - 1)
+    @pl.when(b >= 2)
+    def _():
+        wait_twin(0)
+        update(0, range(PIECES))
+
+    fresh = jnp.where(b >= 2, 1, 0)
+
+    @pl.loop(fresh, b)
     def _(s):
         wait_twin(s)
-        update(s, range(PIECES))
-
-    @pl.when(b > 0)
-    def _():
-        wait_twin(b - 1)
 
     gpart[...] = jnp.zeros_like(gpart)
 
     @pl.loop(0, PIECES)
     def _(j):
-        @pl.when(b > 0)
-        def _():
-            update(b - 1, [j])
+        @pl.loop(fresh, b)
+        def _(s):
+            update(s, [j])
 
         apply_inverse(j)
         for d in range(1, bands):
@@ -370,40 +381,32 @@
         if p != q:
             g_ref[q * rb : (q + 1) * rb, p * rb : (p + 1) * rb] = value.T
 
+    def drained(tile, turn, i, moves, send):
+        s, live = tile(turn)
+        s = jnp.clip(s, 0, last)
+        for wide, on in sizes(s, c, i, live):
+            @pl.when(jnp.logical_and(on, moves))
+            def _():
+                send(s, i, wide).wait_send()
+
+            @pl.when(jnp.logical_and(on, s != z))
+            def _():
+                to_twin(s, i, wide).wait_send()
+
     for turn in range(bands - 1):
         @pl.loop(0, CHUNKS)
         def _(i):
-            s, live = right_tile(turn)
-            s = jnp.clip(s, 0, last)
-            live = jnp.logical_and(live, needed(s, c, i))
-
-            @pl.when(jnp.logical_and(live, z < line - 1))
-            def _():
-                to_right(s, i).wait_send()
-
-            @pl.when(jnp.logical_and(live, s < z))
-            def _():
-                to_twin(s, i).wait_send()
-
-            t, live = left_tile(turn)
-            t = jnp.clip(t, 0, last)
-            live = jnp.logical_and(live, needed(t, c, i))
-
-            @pl.when(jnp.logical_and(live, z > 0))
-            def _():
-                to_left(t, i).wait_send()
-
-            @pl.when(jnp.logical_and(live, t > z))
-            def _():
-                to_twin(t, i).wait_send()
+            drained(right_tile, turn, i, z < line - 1, to_right)
+            drained(left_tile, turn, i, z > 0, to_left)
 
     @pl.when(z <= b)
     def _():
         @pl.loop(0, CHUNKS)
         def _(i):
-            @pl.when(needed(z, c, i))
-            def _():
-                to_twin(z, i).wait_send()
+            for wide, on in sizes(z, c, i):
+                @pl.when(on)
+                def _():
+                    to_twin(z, i, wide).wait_send()
 
     @pl.loop(0, PIECES)
     def _(j):

time: 278 us -> 264 us (0.950)
  Pallas kernels: 272 us -> 258 us
    pallas_call x1, Pallas kernels: 272 us -> 258 us  [local(): pl.pallas_call(functools.partial(kernel, bands, line), out_shape=(jax.Sha...]
where the time goes in v3:
time: 264 us; the launch traced here: 263 us
  Pallas kernels  258 us (98%)
  local copies, waits for them, and re-layouts  5.25 us (2%)
    pallas_call x1, Pallas kernels, local(): pl.pallas_call(functools.partial(kernel, bands, line), out_shape=(jax.Sha...  258 us

profile of v3, /device:TPU:7, one launch (start us, length us, event | category | flops | bytes accessed | tf_op | source)
XLA Modules:
  0.0 263.5 jit_solution(14344214696806093839)
XLA Ops:
  0.6 257.6 %shard_map.41 = (f32[1024,512]{1,0:T(8,128)}, f32[1024,1024]{1,0:T(8,128)}) custom-call(f32[1024,512]{1,0:T(8,128)} %psi_ref.1, f32[1024,512]{1,0:T(8,128)} %low_ref.1), custom_call_target="tpu_custom_call" | custom-call | tf_op jit(solution)/shard_map/pallas_call | solution.py:446
  258.2 0.0 copy-start
  258.2 3.2 %copy.6 = f32[1024,512]{1,0:T(8,128)} copy(f32[1024,512]{1,0:T(8,128)} %get-tuple-element.4) | data formatting | bytes 4194304
  261.5 0.0 copy-done
  261.5 2.0 copy.7
Async XLA Ops:
  258.2 3.2 %copy-start = (f32[1024,1024]{1,0:T(8,128)S(1)}, f32[1024,1024]{1,0:T(8,128)}, u32[]{:S(2)}) copy-start(f32[1024,1024]{1,0:T(8,128)} %get-tuple-element.5) | copy-start | bytes 12582916

commit v4 on v3

--- a/solution.py
+++ b/solution.py
@@ -10,7 +10,7 @@
 MESH = pl.DeviceIdType.MESH
 BASE = 128
 PIECES = 4
-CHUNKS = 8
+CHUNKS = 16
 SKEW = 2
 ROWS = 4
 F32 = jnp.float32

time: 264 us -> 267 us (1.011)
  Pallas kernels: 258 us -> 261 us
    pallas_call x1, Pallas kernels: 258 us -> 261 us  [local(): pl.pallas_call(functools.partial(kernel, bands, line), out_shape=(jax.Sha...]
where the time goes in v4:
time: 267 us
  Pallas kernels  261 us (98%)
  local copies, waits for them, and re-layouts  5.25 us (2%)
    pallas_call x1, Pallas kernels, local(): pl.pallas_call(functools.partial(kernel, bands, line), out_shape=(jax.Sha...  261 us

profile of v4, /device:TPU:7, one launch (start us, length us, event | category | flops | bytes accessed | tf_op | source)
XLA Modules:
  0.0 267.3 jit_solution(5722710607371105395)
XLA Ops:
  0.6 261.4 %shard_map.41 = (f32[1024,512]{1,0:T(8,128)}, f32[1024,1024]{1,0:T(8,128)}) custom-call(f32[1024,512]{1,0:T(8,128)} %psi_ref.1, f32[1024,512]{1,0:T(8,128)} %low_ref.1), custom_call_target="tpu_custom_call" | custom-call | tf_op jit(solution)/shard_map/pallas_call | solution.py:446
  262.0 0.0 copy-start
  262.0 3.2 %copy.6 = f32[1024,512]{1,0:T(8,128)} copy(f32[1024,512]{1,0:T(8,128)} %get-tuple-element.4) | data formatting | bytes 4194304
  265.3 0.0 copy-done
  265.3 2.0 copy.7
Async XLA Ops:
  262.0 3.2 %copy-start = (f32[1024,1024]{1,0:T(8,128)S(1)}, f32[1024,1024]{1,0:T(8,128)}, u32[]{:S(2)}) copy-start(f32[1024,1024]{1,0:T(8,128)} %get-tuple-element.5) | copy-start | bytes 12582916
